TPU v7x, 32 devices: a whole 2x2x4 slice. The times are simulated.
32 devices in a mesh: dp: 8 (over z, y), fsdp: 4 (over x, core).
Axes of the slice: x: 2, y: 2, z: 4, core: 2. Of those that a mesh axis runs over, the one named last changes fastest.
Arguments:
- tokens: bfloat16 [16384, 4096], P(('dp', 'fsdp')), may hold values from -0.75 to 0.75
- doc_ids: int32 [16384], P(('dp', 'fsdp')), may hold values from 0 to 15, never falling along the last dimension, each value on 1 to 2048 neighbouring positions
- attn_gain: float32 [4096], replicated, may hold values from 0.1 to 1.9
- mlp_gain: float32 [4096], replicated, may hold values from 0.1 to 1.9
- w_query: bfloat16 [4096, 512], P(('dp', 'fsdp')), may hold values from -1 to 1
- w_key_value: bfloat16 [4096, 256], P(('dp', 'fsdp')), may hold values from -3 to 3
- w_out: bfloat16 [512, 4096], P(None, ('dp', 'fsdp')), may hold values from -0.25 to 0.25
- w_gate: bfloat16 [4096, 1024], P(('dp', 'fsdp')), may hold values from -0.09375 to 0.09375
- w_up: bfloat16 [4096, 1024], P(('dp', 'fsdp')), may hold values from -0.09375 to 0.09375
- w_down: bfloat16 [1024, 4096], P(None, ('dp', 'fsdp')), may hold values from -0.1875 to 0.1875
Outputs:
- mixed: bfloat16 [16384, 4096], P(('dp', 'fsdp'))
Inputs may be any that keep to these rules, and one draw needn't show every extreme that they name: `doc_ids`: document numbers never fall along the pack, and every document has at most 2048 tokens.
All inputs are finite; a program needn't handle non-finite values.
Results may differ from a plain program's by a relative error of at most 0.02.
The roundings to bfloat16 on the way count: a program that leaves them out, or rounds other values in their place, can miss the bound.
Values may be sent and summed in bfloat16 or wider, within the bound.
A program may use at most 128 MiB of HBM per device.

v0:
```python
import math
import jax
import jax.numpy as jnp
from jax import lax
from jax.sharding import PartitionSpec as P

SPAN = 4
EPS = 1e-05
THETA = 500000.0
NEGATIVE = -1e30


def shifted(array, axis, by):
    length = lax.axis_size(axis)
    pairs = [(i, i + by) for i in range(length) if 0 <= i + by < length]
    return lax.ppermute(array, axis, pairs)


def rms_scale(values, gain):
    wide = values.astype(jnp.float32)
    power = jnp.mean(wide * wide, axis=-1, keepdims=True)
    return (wide * lax.rsqrt(power + EPS) * gain).astype(jnp.bfloat16)


def rotate(values, position):
    head = values.shape[-1]
    half = head // 2
    freqs = THETA ** (-2.0 * jnp.arange(half, dtype=jnp.float32) / head)
    angle = position.astype(jnp.float32)[:, None, None] * freqs[None, None, :]
    cosine = jnp.cos(angle)
    sine = jnp.sin(angle)
    first = values[..., :half]
    second = values[..., half:]
    return jnp.concatenate(
        [first * cosine - second * sine, second * cosine + first * sine], axis=-1
    )


def head_scores(query, keys):
    return jnp.einsum("qhd,kd->hqk", query, keys, preferred_element_type=jnp.float32) / math.sqrt(
        query.shape[-1]
    )


def weigh_values(weights, values):
    return jnp.einsum(
        "hqk,kd->qhd", weights.astype(jnp.bfloat16), values, preferred_element_type=jnp.float32
    )


def attend_dense(query, keys, values, key_marks, marks, offset):
    scores = head_scores(query, keys)
    key_index = jnp.arange(keys.shape[0], dtype=jnp.int32)
    query_index = jnp.arange(query.shape[0], dtype=jnp.int32) + offset
    allowed = (key_marks[None, :] == marks[:, None]) & (key_index[None, :] <= query_index[:, None])
    scores = jnp.where(allowed[None, :, :], scores, NEGATIVE)
    peak = jnp.max(scores, axis=2, keepdims=True)
    weights = jnp.exp(scores - peak)
    totals = jnp.sum(weights, axis=2)
    return weigh_values(weights, values) / jnp.transpose(totals)[:, :, None]


def per_device(
    tokens, doc_ids, attn_gain, mlp_gain, w_query, w_key_value, w_out, w_gate, w_up, w_down
):
    rows = tokens.shape[0]
    rank = lax.axis_index(("dp", "fsdp"))
    normed = rms_scale(tokens, attn_gain)
    query_width = w_query.shape[1]
    pair_width = w_key_value.shape[1]
    head = pair_width // 2
    heads = query_width // head
    group_query, group_pair = (
        lax.all_gather(w_query, "fsdp", axis=0, tiled=True),
        lax.all_gather(w_key_value, "fsdp", axis=0, tiled=True),
    )
    pieces = (
        lax.all_gather(group_query, "dp", axis=0, tiled=True),
        lax.all_gather(group_pair, "dp", axis=0, tiled=True),
    )
    columns = normed
    query_raw = jnp.dot(columns, pieces[0], preferred_element_type=jnp.float32)
    pair_raw = jnp.dot(columns, pieces[1], preferred_element_type=jnp.float32)
    position = rank * rows + jnp.arange(rows, dtype=jnp.int32)
    query = rotate(query_raw.reshape(rows, heads, head), position).astype(jnp.bfloat16)
    keys = rotate(pair_raw[:, None, :head], position)[:, 0, :].astype(jnp.bfloat16)
    values = pair_raw[:, head:].astype(jnp.bfloat16)
    own_pairs = jnp.concatenate([keys, values], axis=1)
    marks = doc_ids + 1
    amounts = [1] + [1 << level for level in range(SPAN.bit_length() - 1)]
    held_pairs = own_pairs
    held_marks = marks
    for order, amount in enumerate(amounts):
        moved_pairs, moved_marks = shifted((held_pairs, held_marks), ("dp", "fsdp"), amount)
        if order == 0:
            held_pairs = moved_pairs
            held_marks = moved_marks
        else:
            held_pairs = jnp.concatenate([moved_pairs, held_pairs], axis=0)
            held_marks = jnp.concatenate([moved_marks, held_marks], axis=0)
    every_pair = jnp.concatenate([held_pairs, own_pairs], axis=0)
    every_mark = jnp.concatenate([held_marks, marks], axis=0)
    mixed = attend_dense(
        query, every_pair[:, :head], every_pair[:, head:], every_mark, marks, held_pairs.shape[0]
    )
    attended = mixed.reshape(rows, query_width).astype(jnp.bfloat16)
    projected = jnp.dot(
        attended,
        lax.all_gather(w_out, ("dp", "fsdp"), axis=1, tiled=True),
        preferred_element_type=jnp.float32,
    )
    resid = (tokens.astype(jnp.float32) + projected).astype(jnp.bfloat16)
    resid = lax.optimization_barrier(resid)
    normed_mlp = rms_scale(resid, mlp_gain)
    pieces = (
        lax.all_gather(w_gate, ("dp", "fsdp"), axis=0, tiled=True),
        lax.all_gather(w_up, ("dp", "fsdp"), axis=0, tiled=True),
    )
    columns = normed_mlp
    gate = jnp.dot(columns, pieces[0], preferred_element_type=jnp.float32)
    up_value = jnp.dot(columns, pieces[1], preferred_element_type=jnp.float32)
    hidden = (jax.nn.silu(gate) * up_value).astype(jnp.bfloat16)
    down = jnp.dot(
        hidden,
        lax.all_gather(w_down, ("dp", "fsdp"), axis=1, tiled=True),
        preferred_element_type=jnp.float32,
    )
    return (resid.astype(jnp.float32) + down).astype(jnp.bfloat16)


def solution(mesh):
    in_specs = (
        P(("dp", "fsdp"), None),
        P(("dp", "fsdp")),
        P(),
        P(),
        P(("dp", "fsdp"), None),
        P(("dp", "fsdp"), None),
        P(None, ("dp", "fsdp")),
        P(("dp", "fsdp"), None),
        P(("dp", "fsdp"), None),
        P(None, ("dp", "fsdp")),
    )
    out_specs = P(("dp", "fsdp"), None)
    return jax.shard_map(
        per_device, mesh=mesh, in_specs=in_specs, out_specs=out_specs, check_vma=False
    )
```

profile of v0, /device:TPU:0, one launch (start us, length us, event | category | flops | bytes accessed | tf_op | source)
XLA Modules:
  0.0 483.1 jit_solution(8188637932389461897)
XLA Ops:
  6.5 9.0 %all_gather.24 = bf16[512,256]{1,0:T(8,128)(2,1)} all-gather(bf16[128,256]{1,0:T(8,128)(2,1)} %param.15), channel_id=1, replica_groups=mesh['dp'=8,'fsdp'=4] {'fsdp'}, dimensions={0}, use_global_device_ids=true | all-gather | bytes 327680 | tf_op jit(solution)/shard_map/all_gather | solution.py:75
  15.6 8.3 %all_gather.26 = bf16[512,512]{1,0:T(8,128)(2,1)} all-gather(bf16[128,512]{1,0:T(8,128)(2,1)} %param.14), channel_id=1, replica_groups=mesh['dp'=8,'fsdp'=4] {'fsdp'}, dimensions={0}, use_global_device_ids=true | all-gather | bytes 655360 | tf_op jit(solution)/shard_map/all_gather | solution.py:74
  26.4 3.1 fusion.6
  29.5 35.6 %all-gather.7.cloned.1.call-done = bf16[4096,256]{1,0:T(8,128)(2,1)} async-done(((bf16[512,256]{1,0:T(8,128)(2,1)}), bf16[4096,256]{1,0:T(8,128)(2,1)}) %all-gather.7.cloned.1.call-update) | async-done | bytes 2097168 | tf_op jit(solution)/shard_map/all_gather | solution.py:79
  65.1 4.4 fusion.23
  71.5 4.1 collective-permute-start.3
  76.4 2.5 collective-permute-start.4
  79.9 4.4 collective-permute-start.1
  84.4 3.4 collective-permute-start.5
  89.2 4.4 collective-permute-start.2
  95.0 10.2 %collective-permute-done.2 = bf16[1024,256]{0,1:T(8,128)(2,1)S(1)} collective-permute-done((bf16[1024,256]{0,1:T(8,128)(2,1)S(1)}, bf16[1024,256]{0,1:T(8,128)(2,1)S(1)}, u32[]{:S(2)}, u32[]{:S(2)}) %collective-permute-start.2) | collective-permute-done | bytes 524320 | tf_op jit(solution)/shard_map/ppermute | solution.py:16
  106.4 44.8 %all-gather.9.cloned.1.call-done = bf16[4096,512]{1,0:T(8,128)(2,1)} async-done(((bf16[512,512]{1,0:T(8,128)(2,1)}), bf16[4096,512]{1,0:T(8,128)(2,1)}) %all-gather.9.cloned.1.call-update) | async-done | bytes 4194320 | tf_op jit(solution)/shard_map/all_gather | solution.py:78
  151.2 5.9 %fusion.21 = f32[512,512]{0,1:T(8,128)S(1)} fusion(bf16[4096,512]{1,0:T(8,128)(2,1)} %all-gather.9.cloned.1.call-done, bf16[512,4096]{1,0:T(8,128)(2,1)} %param.10, f32[4096]{0:T(1024)S(1)} %copy-done.3, f32[512]{0:T(512)S(1)} %add_rsqrt_fusion.1), kind=kOutput, calls=%fused_computation.27 | convolution fusion | flops 2155872256 | bytes 9455616 | tf_op jit(solution)/shard_map/dot_general | solution.py:82
  162.4 5.3 %fusion.2 = (f32[4,512]{1,0:T(4,128)S(1)}, f32[2560,512,4]{1,0,2:T(8,128)S(1)}) fusion(pred[512,2560]{0,1:T(8,128)(4,1)S(1)} %fusion.14, bf16[512,4,64]{2,0,1:T(8,128)(2,1)S(1)} %get-tuple-element.6, bf16[512,4,64]{2,0,1:T(8,128)(2,1)S(1)} %get-tuple-element.5, bf16[2560,256]{0,1:T(8,128)(2,1)} %maximum_maximum_fusion), kind=kOutput, calls=%fused_computation.4 | convolution fusion | flops 1358952448 | bytes 23470080 | tf_op jit(solution)/shard_map/qhd,kd->hqk/dot_general | solution.py:40
  167.6 4.5 fusion
  172.2 6.1 %divide_convert_fusion = bf16[512,4,128]{0,2,1:T(8,128)(2,1)S(1)} fusion(f32[2560,512,4]{1,0,2:T(8,128)S(1)} %get-tuple-element.14, f32[4,512]{1,0:T(4,128)S(1)} %get-tuple-element.13, pred[512,2560]{0,1:T(8,128)(4,1)S(1)} %fusion.14, bf16[2560,256]{0,1:T(8,128)(2,1)S(1)} %copy-done.1, f32[512,4]{0,1:T(4,128)S(1)} %bitcast.42), kind=kOutput, calls=%fused_computation.29 | convolution fusion | flops 1363673088 | bytes 23478272 | tf_op jit(solution)/shard_map/hqk,kd->qhd/dot_general | solution.py:46
  178.3 38.3 %all-gather.11.cloned.1.call-done = bf16[512,4096]{1,0:T(8,128)(2,1)} async-done(((bf16[512,128]{1,0:T(8,128)(2,1)}), bf16[512,4096]{1,0:T(8,128)(2,1)}) %all-gather.11.cloned.1.call-update) | async-done | bytes 4194320 | tf_op jit(solution)/shard_map/all_gather | solution.py:109
  216.7 5.9 %fusion.9 = bf16[512,4096]{1,0:T(8,128)(2,1)S(1)} fusion(bf16[512,4096]{1,0:T(8,128)(2,1)} %param.10, bf16[512,512]{0,1:T(8,128)(2,1)S(1)} %bitcast.41, bf16[512,4096]{1,0:T(8,128)(2,1)} %all-gather.11.cloned.1.call-done), kind=kOutput, calls=%fused_computation.16 | convolution fusion | flops 2153775104 | bytes 13107200 | tf_op jit(solution)/shard_map/dot_general | solution.py:107
  225.5 69.2 %all-gather.13.cloned.1.call-done = bf16[4096,1024]{1,0:T(8,128)(2,1)} async-done(((bf16[128,1024]{1,0:T(8,128)(2,1)}), bf16[4096,1024]{1,0:T(8,128)(2,1)}) %all-gather.13.cloned.1.call-update) | async-done | bytes 8388624 | tf_op jit(solution)/shard_map/all_gather | solution.py:116
  294.6 8.2 %fusion.19 = f32[512,1024]{1,0:T(8,128)S(1)} fusion(bf16[4096,1024]{1,0:T(8,128)(2,1)} %all-gather.13.cloned.1.call-done, bf16[512,4096]{1,0:T(8,128)(2,1)} %copy-done, f32[4096]{0:T(1024)S(1)} %copy-done.4, f32[512]{0:T(512)S(1)} %add_rsqrt_fusion), kind=kOutput, calls=%fused_computation.26 | convolution fusion | flops 4303355904 | bytes 14698496 | tf_op jit(solution)/shard_map/dot_general | solution.py:120
  302.9 70.2 %all-gather.15.cloned.1.call-done = bf16[4096,1024]{1,0:T(8,128)(2,1)} async-done(((bf16[128,1024]{1,0:T(8,128)(2,1)}), bf16[4096,1024]{1,0:T(8,128)(2,1)}) %all-gather.15.cloned.1.call-update) | async-done | bytes 8388624 | tf_op jit(solution)/shard_map/all_gather | solution.py:117
  373.0 9.4 %multiply_convert_fusion = bf16[512,1024]{1,0:T(8,128)(2,1)S(1)} fusion(f32[512,1024]{1,0:T(8,128)S(1)} %fusion.19, bf16[4096,1024]{1,0:T(8,128)(2,1)} %all-gather.15.cloned.1.call-done, bf16[512,4096]{1,0:T(8,128)(2,1)} %copy-done, f32[4096]{0:T(1024)S(1)} %copy-done.4, f32[512]{0:T(512)S(1)} %add_rsqrt_fusion), kind=kOutput, calls=%fused_computation.23 | convolution fusion | flops 4306501632 | bytes 15747072 | tf_op jit(solution)/shard_map/dot_general | solution.py:121
  382.4 83.8 %all-gather.17.cloned.1.call-done = bf16[1024,4096]{1,0:T(8,128)(2,1)} async-done(((bf16[1024,128]{1,0:T(8,128)(2,1)}), bf16[1024,4096]{1,0:T(8,128)(2,1)}) %all-gather.17.cloned.1.call-update) | async-done | bytes 8388624 | tf_op jit(solution)/shard_map/all_gather | solution.py:125
  466.2 10.1 %fusion.13 = bf16[512,4096]{1,0:T(8,128)(2,1)} fusion(bf16[512,4096]{1,0:T(8,128)(2,1)} %copy-done, bf16[512,1024]{1,0:T(8,128)(2,1)S(1)} %multiply_convert_fusion, bf16[1024,4096]{1,0:T(8,128)(2,1)} %all-gather.17.cloned.1.call-done), kind=kOutput, calls=%fused_computation.20 | convolution fusion | flops 4301258752 | bytes 17825792 | tf_op jit(solution)/shard_map/dot_general | solution.py:123
  (50 shorter events, 18.3 us)
Async XLA Ops:
  6.5 58.6 %copy-start.3 = (f32[4096]{0:T(1024)S(1)}, f32[4096]{0:T(1024)}, u32[]{:S(2)}) copy-start(f32[4096]{0:T(1024)} %param.12) | copy-start | bytes 49156
  6.5 58.5 %all-gather.7.cloned.1.call-start = ((), (), s32[]{:S(2)}) async-start(), calls=%async_computation | async-start | bytes 2359296 | tf_op jit(solution)/shard_map/all_gather | solution.py:79
  15.5 135.7 %all-gather.9.cloned.1.call-start = ((), (), s32[]{:S(2)}) async-start(), calls=%async_computation.1 | async-start | bytes 4718592 | tf_op jit(solution)/shard_map/all_gather | solution.py:78
  23.9 192.8 %all-gather.11.cloned.1.call-start = ((), (), s32[]{:S(2)}) async-start(), calls=%async_computation.2 | async-start | bytes 4325376 | tf_op jit(solution)/shard_map/all_gather | solution.py:109
  24.6 270.0 %all-gather.13.cloned.1.call-start = ((), (), s32[]{:S(2)}) async-start(), calls=%async_computation.3 | async-start | bytes 8650752 | tf_op jit(solution)/shard_map/all_gather | solution.py:116
  25.2 347.8 %all-gather.15.cloned.1.call-start = ((), (), s32[]{:S(2)}) async-start(), calls=%async_computation.4 | async-start | bytes 8650752 | tf_op jit(solution)/shard_map/all_gather | solution.py:117
  25.8 440.4 %all-gather.17.cloned.1.call-start = ((), (), s32[]{:S(2)}) async-start(), calls=%async_computation.5 | async-start | bytes 8650752 | tf_op jit(solution)/shard_map/all_gather | solution.py:125
  29.5 42.0 %copy-start.2 = (s32[512]{0:T(512)S(1)}, s32[512]{0:T(512)}, u32[]{:S(2)}) copy-start(s32[512]{0:T(512)} %param.11) | copy-start | bytes 6148
  70.2 9.7 %collective-permute-start = (bf16[512,256]{0,1:T(8,128)(2,1)S(1)}, bf16[512,256]{0,1:T(8,128)(2,1)S(1)}, u32[]{:S(2)}, u32[]{:S(2)}) collective-permute-start(bf16[512,256]{0,1:T(8,128)(2,1)S(1)} %pad_maximum_fusion.1), channel_id=1, source_target_pairs={{0,1},{1,2},{2,3},{3,4},{4,5},{5,6},{6,7},{7,8},{8,9},{9,10},{10,1... | collective-permute-start | bytes 786440 | tf_op jit(solution)/shard_map/ppermute | solution.py:16
  71.5 4.9 %collective-permute-start.3 = (s32[512]{0:T(512)S(1)}, s32[512]{0:T(512)S(1)}, u32[]{:S(2)}, u32[]{:S(2)}) collective-permute-start(s32[512]{0:T(512)S(1)} %broadcast_add_fusion), channel_id=1, source_target_pairs={{0,1},{1,2},{2,3},{3,4},{4,5},{5,6},{6,7},{7,8},{8,9},{9,10},{10,1... | collective-permute-start | bytes 6152 | tf_op jit(solution)/shard_map/ppermute | solution.py:16
  76.4 7.9 %collective-permute-start.4 = (s32[512]{0:T(512)S(1)}, s32[512]{0:T(512)S(1)}, u32[]{:S(2)}, u32[]{:S(2)}) collective-permute-start(s32[512]{0:T(512)S(1)} %collective-permute-done.3), channel_id=1, source_target_pairs={{0,1},{1,2},{2,3},{3,4},{4,5},{5,6},{6,7},{7,8},{8,9},{9,10},{10,1... | collective-permute-start | bytes 6152 | tf_op jit(solution)/shard_map/ppermute | solution.py:16
  79.9 9.2 %collective-permute-start.1 = (bf16[512,256]{0,1:T(8,128)(2,1)S(1)}, bf16[512,256]{0,1:T(8,128)(2,1)S(1)}, u32[]{:S(2)}, u32[]{:S(2)}) collective-permute-start(bf16[512,256]{0,1:T(8,128)(2,1)S(1)} %collective-permute-done), channel_id=1, source_target_pairs={{0,1},{1,2},{2,3},{3,4},{4,5},{5,6},{6,7},{7,8},{8,9},{9,10},{10,1... | collective-permute-start | bytes 786440 | tf_op jit(solution)/shard_map/ppermute | solution.py:16
  84.4 4.8 collective-permute-start.5
  89.2 16.1 %collective-permute-start.2 = (bf16[1024,256]{0,1:T(8,128)(2,1)S(1)}, bf16[1024,256]{0,1:T(8,128)(2,1)S(1)}, u32[]{:S(2)}, u32[]{:S(2)}) collective-permute-start(bf16[1024,256]{0,1:T(8,128)(2,1)S(1)} %pad_maximum_fusion), channel_id=1, source_target_pairs={{0,2},{1,3},{2,4},{3,5},{4,6},{5,7},{6,8},{7,9},{8,10},{9,11},{10,... | collective-permute-start | bytes 1572872 | tf_op jit(solution)/shard_map/ppermute | solution.py:16
  167.6 4.6 copy-start.1
  222.6 2.0 copy-start
  224.6 70.1 %copy-start.4 = (f32[4096]{0:T(1024)S(1)}, f32[4096]{0:T(1024)}, u32[]{:S(2)}) copy-start(f32[4096]{0:T(1024)} %param.13) | copy-start | bytes 49156
Sparse Core Ops, SparseCore 0:
  15.6 49.3 all-gather.6
  67.2 83.9 all-gather.8
  154.0 62.5 all-gather.10
  219.4 75.2 all-gather.12
  297.3 75.6 all-gather.14
  375.8 90.4 all-gather.16
where the time goes:
time: 484 us; the launch traced here: 483 us
  waiting for transfers between devices  356 us (74%)
  matrix products  55.3 us (11%)
  starting transfers between devices  20.3 us (4%)
  blocking collectives  17.3 us (4%)
  other arithmetic  14.3 us (3%)
  between operations  13.7 us (3%)
  local copies, waits for them, and re-layouts  5.75 us (1%)
    all_gather x1, waiting for transfers between devices, per_device(): lax.all_gather(w_down, ('dp', 'fsdp'), axis=1, tiled=True)  83.8 us
    all_gather x1, waiting for transfers between devices, per_device(): lax.all_gather(w_up, ('dp', 'fsdp'), axis=0, tiled=True)  70.2 us
    all_gather x1, waiting for transfers between devices, per_device(): lax.all_gather(w_gate, ('dp', 'fsdp'), axis=0, tiled=True)  69.2 us
    all_gather x1, waiting for transfers between devices, per_device(): lax.all_gather(group_query, 'dp', axis=0, tiled=True)  44.8 us
    all_gather x1, waiting for transfers between devices, per_device(): lax.all_gather(w_out, ('dp', 'fsdp'), axis=1, tiled=True)  38.3 us
    all_gather x1, waiting for transfers between devices, per_device(): lax.all_gather(group_pair, 'dp', axis=0, tiled=True)  35.6 us
    ppermute x6, starting transfers between devices, shifted(): return lax.ppermute(array, axis, pairs)  20.1 us
    ppermute x6, waiting for transfers between devices, shifted(): return lax.ppermute(array, axis, pairs)  12.3 us
  transfers between devices with their start and end apart: 12, of which 9 were waited for; matrix products, arithmetic and copies ran while one was open for 13% of the time, Pallas kernels for 0%

commit v1 on v0

--- a/solution.py
+++ b/solution.py
@@ -1,3 +1,4 @@
+import functools
 import math
 import jax
 import jax.numpy as jnp
@@ -8,6 +9,14 @@
 EPS = 1e-05
 THETA = 500000.0
 NEGATIVE = -1e30
+
+
+def windows_trace(local_block, chip_axis, dim_at):
+    carry = jnp.concatenate(jax.lax.all_gather(local_block, chip_axis), dim_at)
+    return carry
+
+
+page_carry = functools.partial(windows_trace, chip_axis=("dp", "fsdp"), dim_at=1)
 
 
 def shifted(array, axis, by):
@@ -120,11 +129,7 @@
     gate = jnp.dot(columns, pieces[0], preferred_element_type=jnp.float32)
     up_value = jnp.dot(columns, pieces[1], preferred_element_type=jnp.float32)
     hidden = (jax.nn.silu(gate) * up_value).astype(jnp.bfloat16)
-    down = jnp.dot(
-        hidden,
-        lax.all_gather(w_down, ("dp", "fsdp"), axis=1, tiled=True),
-        preferred_element_type=jnp.float32,
-    )
+    down = jnp.dot(hidden, page_carry(w_down), preferred_element_type=jnp.float32)
     return (resid.astype(jnp.float32) + down).astype(jnp.bfloat16)
 
 

time: 484 us -> 477 us (0.986)
  waiting for transfers between devices: 356 us -> 337 us
  local copies, waits for them, and re-layouts: 5.75 us -> 17.1 us
    all_gather x1, waiting for transfers between devices: 83.8 us -> 69.2 us  [windows_trace(): carry = jnp.concatenate(jax.lax.all_gather(local_block, chip_axis), dim_at)]
    reshape x0 -> x1, local copies, waits for them, and re-layouts: none -> 11.3 us  [windows_trace(): carry = jnp.concatenate(jax.lax.all_gather(local_block, chip_axis), dim_at)]
  transfers between devices with their start and end apart: 12 -> 12, of which waited for: 9 -> 9; matrix products, arithmetic and copies ran while one was open for 13% -> 14% of each run, Pallas kernels for 0% -> 0%
where the time goes in v1:
time: 477 us
  waiting for transfers between devices  337 us (71%)
  matrix products  56.5 us (12%)
  starting transfers between devices  20.3 us (4%)
  blocking collectives  17.3 us (4%)
  local copies, waits for them, and re-layouts  17.1 us (4%)
  other arithmetic  14.3 us (3%)
  between operations  13.7 us (3%)
    all_gather x1, waiting for transfers between devices, windows_trace(): carry = jnp.concatenate(jax.lax.all_gather(local_block, chip_axis), dim_at)  69.2 us
    all_gather x1, waiting for transfers between devices, per_device(): lax.all_gather(w_up, ('dp', 'fsdp'), axis=0, tiled=True)  67.9 us
    all_gather x1, waiting for transfers between devices, per_device(): lax.all_gather(w_gate, ('dp', 'fsdp'), axis=0, tiled=True)  67.1 us
    all_gather x1, waiting for transfers between devices, per_device(): lax.all_gather(group_query, 'dp', axis=0, tiled=True)  44.8 us
    all_gather x1, waiting for transfers between devices, per_device(): lax.all_gather(w_out, ('dp', 'fsdp'), axis=1, tiled=True)  38.3 us
    all_gather x1, waiting for transfers between devices, per_device(): lax.all_gather(group_pair, 'dp', axis=0, tiled=True)  35.6 us
    ppermute x6, starting transfers between devices, shifted(): return lax.ppermute(array, axis, pairs)  20.1 us
    ppermute x6, waiting for transfers between devices, shifted(): return lax.ppermute(array, axis, pairs)  12.3 us
  transfers between devices with their start and end apart: 12, of which 9 were waited for; matrix products, arithmetic and copies ran while one was open for 14% of the time, Pallas kernels for 0%

profile of v1, /device:TPU:0, one launch (start us, length us, event | category | flops | bytes accessed | tf_op | source)
XLA Modules:
  0.0 476.6 jit_solution(5528601957117688253)
XLA Ops:
  6.5 9.0 %all_gather.27 = bf16[512,256]{1,0:T(8,128)(2,1)} all-gather(bf16[128,256]{1,0:T(8,128)(2,1)} %param.15), channel_id=1, replica_groups=mesh['dp'=8,'fsdp'=4] {'fsdp'}, dimensions={0}, use_global_device_ids=true | all-gather | bytes 327680 | tf_op jit(solution)/shard_map/all_gather | solution.py:84
  15.6 8.3 %all_gather.29 = bf16[512,512]{1,0:T(8,128)(2,1)} all-gather(bf16[128,512]{1,0:T(8,128)(2,1)} %param.14), channel_id=1, replica_groups=mesh['dp'=8,'fsdp'=4] {'fsdp'}, dimensions={0}, use_global_device_ids=true | all-gather | bytes 655360 | tf_op jit(solution)/shard_map/all_gather | solution.py:83
  26.4 3.1 fusion.6
  29.5 35.6 %all-gather.8.cloned.1.call-done = bf16[4096,256]{1,0:T(8,128)(2,1)} async-done(((bf16[512,256]{1,0:T(8,128)(2,1)}), bf16[4096,256]{1,0:T(8,128)(2,1)}) %all-gather.8.cloned.1.call-update) | async-done | bytes 2097168 | tf_op jit(solution)/shard_map/all_gather | solution.py:88
  65.1 4.4 fusion.23
  71.5 4.1 collective-permute-start.3
  79.9 4.4 collective-permute-start.1
  84.4 3.4 collective-permute-start.5
  89.2 4.4 collective-permute-start.2
  95.0 10.2 %collective-permute-done.2 = bf16[1024,256]{0,1:T(8,128)(2,1)S(1)} collective-permute-done((bf16[1024,256]{0,1:T(8,128)(2,1)S(1)}, bf16[1024,256]{0,1:T(8,128)(2,1)S(1)}, u32[]{:S(2)}, u32[]{:S(2)}) %collective-permute-start.2) | collective-permute-done | bytes 524320 | tf_op jit(solution)/shard_map/ppermute | solution.py:25
  106.3 44.8 %all-gather.10.cloned.1.call-done = bf16[4096,512]{1,0:T(8,128)(2,1)} async-done(((bf16[512,512]{1,0:T(8,128)(2,1)}), bf16[4096,512]{1,0:T(8,128)(2,1)}) %all-gather.10.cloned.1.call-update) | async-done | bytes 4194320 | tf_op jit(solution)/shard_map/all_gather | solution.py:87
  151.2 5.9 %fusion.21 = f32[512,512]{0,1:T(8,128)S(1)} fusion(bf16[4096,512]{1,0:T(8,128)(2,1)} %all-gather.10.cloned.1.call-done, bf16[512,4096]{1,0:T(8,128)(2,1)} %param.10, f32[4096]{0:T(1024)S(1)} %copy-done.5, f32[512]{0:T(512)S(1)} %add_rsqrt_fusion.1), kind=kOutput, calls=%fused_computation.27 | convolution fusion | flops 2155872256 | bytes 9455616 | tf_op jit(solution)/shard_map/dot_general | solution.py:91
  162.3 5.3 %fusion.2 = (f32[4,512]{1,0:T(4,128)S(1)}, f32[2560,512,4]{1,0,2:T(8,128)S(1)}) fusion(pred[512,2560]{0,1:T(8,128)(4,1)S(1)} %fusion.14, bf16[512,4,64]{2,0,1:T(8,128)(2,1)S(1)} %get-tuple-element.6, bf16[512,4,64]{2,0,1:T(8,128)(2,1)S(1)} %get-tuple-element.5, bf16[2560,256]{0,1:T(8,128)(2,1)} %maximum_maximum_fusion), kind=kOutput, calls=%fused_computation.4 | convolution fusion | flops 1358952448 | bytes 23470080 | tf_op jit(solution)/shard_map/qhd,kd->hqk/dot_general | solution.py:49
  167.6 4.5 fusion
  172.2 6.1 %divide_convert_fusion = bf16[512,4,128]{0,2,1:T(8,128)(2,1)S(1)} fusion(f32[2560,512,4]{1,0,2:T(8,128)S(1)} %get-tuple-element.14, f32[4,512]{1,0:T(4,128)S(1)} %get-tuple-element.13, pred[512,2560]{0,1:T(8,128)(4,1)S(1)} %fusion.14, bf16[2560,256]{0,1:T(8,128)(2,1)S(1)} %copy-done.3, f32[512,4]{0,1:T(4,128)S(1)} %bitcast.48), kind=kOutput, calls=%fused_computation.29 | convolution fusion | flops 1363673088 | bytes 23478272 | tf_op jit(solution)/shard_map/hqk,kd->qhd/dot_general | solution.py:55
  178.3 38.3 %all-gather.12.cloned.1.call-done = bf16[512,4096]{1,0:T(8,128)(2,1)} async-done(((bf16[512,128]{1,0:T(8,128)(2,1)}), bf16[512,4096]{1,0:T(8,128)(2,1)}) %all-gather.12.cloned.1.call-update) | async-done | bytes 4194320 | tf_op jit(solution)/shard_map/all_gather | solution.py:118
  216.7 5.9 %fusion.9 = bf16[512,4096]{1,0:T(8,128)(2,1)S(1)} fusion(bf16[512,4096]{1,0:T(8,128)(2,1)} %param.10, bf16[512,512]{0,1:T(8,128)(2,1)S(1)} %bitcast.47, bf16[512,4096]{1,0:T(8,128)(2,1)} %all-gather.12.cloned.1.call-done), kind=kOutput, calls=%fused_computation.16 | convolution fusion | flops 2153775104 | bytes 13107200 | tf_op jit(solution)/shard_map/dot_general | solution.py:116
  225.5 69.2 %all-gather.18.cloned.1.call-done = bf16[32768,128]{1,0:T(8,128)(2,1)} async-done(((bf16[1024,128]{1,0:T(8,128)(2,1)}), bf16[32768,128]{1,0:T(8,128)(2,1)}) %all-gather.18.cloned.1.call-update) | async-done | bytes 8388624 | tf_op jit(solution)/shard_map/all_gather | solution.py:15
  294.6 11.3 %copy.23 = bf16[1024,32,128]{0,2,1:T(8,128)(2,1)} copy(bf16[1024,32,128]{2,0,1:T(8,128)(2,1)} %bitcast.44) | data formatting | bytes 16777216 | tf_op jit(solution)/shard_map/reshape | solution.py:15
  305.9 67.1 %all-gather.14.cloned.1.call-done = bf16[4096,1024]{1,0:T(8,128)(2,1)} async-done(((bf16[128,1024]{1,0:T(8,128)(2,1)}), bf16[4096,1024]{1,0:T(8,128)(2,1)}) %all-gather.14.cloned.1.call-update) | async-done | bytes 8388624 | tf_op jit(solution)/shard_map/all_gather | solution.py:125
  373.0 10.5 %fusion.19 = f32[512,1024]{1,0:T(8,128)} fusion(bf16[4096,1024]{1,0:T(8,128)(2,1)} %all-gather.14.cloned.1.call-done, bf16[512,4096]{1,0:T(8,128)(2,1)} %copy-done, f32[4096]{0:T(1024)S(1)} %copy-done.6, f32[512]{0:T(512)S(1)} %add_rsqrt_fusion), kind=kOutput, calls=%fused_computation.26 | convolution fusion | flops 4303355904 | bytes 14698496 | tf_op jit(solution)/shard_map/dot_general | solution.py:129
  383.6 67.9 %all-gather.16.cloned.1.call-done = bf16[4096,1024]{1,0:T(8,128)(2,1)} async-done(((bf16[128,1024]{1,0:T(8,128)(2,1)}), bf16[4096,1024]{1,0:T(8,128)(2,1)}) %all-gather.16.cloned.1.call-update) | async-done | bytes 8388624 | tf_op jit(solution)/shard_map/all_gather | solution.py:126
  451.5 11.0 %multiply_convert_fusion = bf16[512,1024]{1,0:T(8,128)(2,1)} fusion(f32[512,1024]{1,0:T(8,128)} %fusion.19, bf16[4096,1024]{1,0:T(8,128)(2,1)} %all-gather.16.cloned.1.call-done, bf16[512,4096]{1,0:T(8,128)(2,1)} %copy-done, f32[4096]{0:T(1024)S(1)} %copy-done.6, f32[512]{0:T(512)S(1)} %add_rsqrt_fusion), kind=kOutput, calls=%fused_computation.23 | convolution fusion | flops 4306501632 | bytes 15747072 | tf_op jit(solution)/shard_map/dot_general | solution.py:130
  462.4 7.3 %fusion.13 = bf16[512,4096]{1,0:T(8,128)(2,1)} fusion(bf16[512,4096]{1,0:T(8,128)(2,1)S(1)} %copy-done.1, bf16[512,1024]{1,0:T(8,128)(2,1)} %multiply_convert_fusion, bf16[1024,4096]{0,1:T(8,128)(2,1)S(1)} %bitcast.45), kind=kOutput, calls=%fused_computation.20 | convolution fusion | flops 4301258752 | bytes 17825792 | tf_op jit(solution)/shard_map/dot_general | solution.py:132
  (55 shorter events, 20.8 us)
Async XLA Ops:
  6.5 58.6 %copy-start.5 = (f32[4096]{0:T(1024)S(1)}, f32[4096]{0:T(1024)}, u32[]{:S(2)}) copy-start(f32[4096]{0:T(1024)} %param.12) | copy-start | bytes 49156
  6.5 58.6 %all-gather.8.cloned.1.call-start = ((), (), s32[]{:S(2)}) async-start(), calls=%async_computation | async-start | bytes 2359296 | tf_op jit(solution)/shard_map/all_gather | solution.py:88
  15.5 135.7 %all-gather.10.cloned.1.call-start = ((), (), s32[]{:S(2)}) async-start(), calls=%async_computation.1 | async-start | bytes 4718592 | tf_op jit(solution)/shard_map/all_gather | solution.py:87
  23.9 192.8 %all-gather.12.cloned.1.call-start = ((), (), s32[]{:S(2)}) async-start(), calls=%async_computation.2 | async-start | bytes 4325376 | tf_op jit(solution)/shard_map/all_gather | solution.py:118
  24.6 270.0 %all-gather.18.cloned.1.call-start = ((), (), s32[]{:S(2)}) async-start(), calls=%async_computation.5 | async-start | bytes 8650752 | tf_op jit(solution)/shard_map/all_gather | solution.py:15
  25.2 347.8 %all-gather.14.cloned.1.call-start = ((), (), s32[]{:S(2)}) async-start(), calls=%async_computation.3 | async-start | bytes 8650752 | tf_op jit(solution)/shard_map/all_gather | solution.py:125
  25.8 425.7 %all-gather.16.cloned.1.call-start = ((), (), s32[]{:S(2)}) async-start(), calls=%async_computation.4 | async-start | bytes 8650752 | tf_op jit(solution)/shard_map/all_gather | solution.py:126
  29.5 42.0 %copy-start.4 = (s32[512]{0:T(512)S(1)}, s32[512]{0:T(512)}, u32[]{:S(2)}) copy-start(s32[512]{0:T(512)} %param.11) | copy-start | bytes 6148
  70.2 9.7 %collective-permute-start = (bf16[512,256]{0,1:T(8,128)(2,1)S(1)}, bf16[512,256]{0,1:T(8,128)(2,1)S(1)}, u32[]{:S(2)}, u32[]{:S(2)}) collective-permute-start(bf16[512,256]{0,1:T(8,128)(2,1)S(1)} %pad_maximum_fusion.1), channel_id=1, source_target_pairs={{0,1},{1,2},{2,3},{3,4},{4,5},{5,6},{6,7},{7,8},{8,9},{9,10},{10,1... | collective-permute-start | bytes 786440 | tf_op jit(solution)/shard_map/ppermute | solution.py:25
  71.5 4.9 %collective-permute-start.3 = (s32[512]{0:T(512)S(1)}, s32[512]{0:T(512)S(1)}, u32[]{:S(2)}, u32[]{:S(2)}) collective-permute-start(s32[512]{0:T(512)S(1)} %broadcast_add_fusion), channel_id=1, source_target_pairs={{0,1},{1,2},{2,3},{3,4},{4,5},{5,6},{6,7},{7,8},{8,9},{9,10},{10,1... | collective-permute-start | bytes 6152 | tf_op jit(solution)/shard_map/ppermute | solution.py:25
  76.4 7.9 %collective-permute-start.4 = (s32[512]{0:T(512)S(1)}, s32[512]{0:T(512)S(1)}, u32[]{:S(2)}, u32[]{:S(2)}) collective-permute-start(s32[512]{0:T(512)S(1)} %collective-permute-done.3), channel_id=1, source_target_pairs={{0,1},{1,2},{2,3},{3,4},{4,5},{5,6},{6,7},{7,8},{8,9},{9,10},{10,1... | collective-permute-start | bytes 6152 | tf_op jit(solution)/shard_map/ppermute | solution.py:25
  79.9 9.2 %collective-permute-start.1 = (bf16[512,256]{0,1:T(8,128)(2,1)S(1)}, bf16[512,256]{0,1:T(8,128)(2,1)S(1)}, u32[]{:S(2)}, u32[]{:S(2)}) collective-permute-start(bf16[512,256]{0,1:T(8,128)(2,1)S(1)} %collective-permute-done), channel_id=1, source_target_pairs={{0,1},{1,2},{2,3},{3,4},{4,5},{5,6},{6,7},{7,8},{8,9},{9,10},{10,1... | collective-permute-start | bytes 786440 | tf_op jit(solution)/shard_map/ppermute | solution.py:25
  84.4 4.8 collective-permute-start.5
  89.2 16.0 %collective-permute-start.2 = (bf16[1024,256]{0,1:T(8,128)(2,1)S(1)}, bf16[1024,256]{0,1:T(8,128)(2,1)S(1)}, u32[]{:S(2)}, u32[]{:S(2)}) collective-permute-start(bf16[1024,256]{0,1:T(8,128)(2,1)S(1)} %pad_maximum_fusion), channel_id=1, source_target_pairs={{0,2},{1,3},{2,4},{3,5},{4,6},{5,7},{6,8},{7,9},{8,10},{9,11},{10,... | collective-permute-start | bytes 1572872 | tf_op jit(solution)/shard_map/ppermute | solution.py:25
  167.6 4.6 copy-start.3
  222.5 2.0 copy-start
  294.6 78.4 %copy-start.6 = (f32[4096]{0:T(1024)S(1)}, f32[4096]{0:T(1024)}, u32[]{:S(2)}) copy-start(f32[4096]{0:T(1024)} %param.13) | copy-start | bytes 49156
  451.5 11.0 %copy-start.1 = (bf16[512,4096]{1,0:T(8,128)(2,1)S(1)}, bf16[512,4096]{1,0:T(8,128)(2,1)}, u32[]{:S(2)}) copy-start(bf16[512,4096]{1,0:T(8,128)(2,1)} %copy-done) | copy-start | bytes 12582916
  451.5 11.0 %copy-start.2 = (bf16[1024,32,128]{0,2,1:T(8,128)(2,1)S(1)}, bf16[1024,32,128]{0,2,1:T(8,128)(2,1)}, u32[]{:S(2)}) copy-start(bf16[1024,32,128]{0,2,1:T(8,128)(2,1)} %copy.23) | copy-start | bytes 25165828
Sparse Core Ops, SparseCore 0:
  15.6 49.3 all-gather.7
  67.2 83.9 all-gather.9
  154.0 62.5 all-gather.11
  219.4 75.2 all-gather.17
  297.3 75.6 all-gather.13
  375.7 75.6 all-gather.15
